TPU v7x, 32 devices: a whole 2x2x4 slice. The times are simulated.
32 devices in a mesh: gx: 16 (over z, x, core), gy: 2 (over y).
Axes of the slice: x: 2, y: 2, z: 4, core: 2. Of those that a mesh axis runs over, the one named last changes fastest.
Arguments:
- velocity: float32 [256, 256, 512], P('gx', 'gy'), may hold values from -24 to 24
- viscosity: float32 [256], P('gx'), may hold values from 1000 to 8000
- marker_forces: bfloat16 [4096, 16], P(('gx', 'gy')), may hold values from -18 to 18
- spread_weights: bfloat16 [4096, 16, 2048], P(('gx', 'gy')), may hold values from -1.5 to 1.5
- block_owner: int32 [4096, 1], P(('gx', 'gy')), may hold values from 0 to 31; in each aligned block of 128 rows (0 to 127, 128 to 255, ...) at most 8 rows name the same one
- tile_slot: int32 [4096], P(('gx', 'gy')), may hold values from 0 to 511
Outputs:
- relaxed: float32 [256, 256, 512], P('gx', 'gy')
Inputs may be any that keep to these rules, and one draw needn't show every extreme that they name: `block_owner`: among the 128 blocks held by one device, no owner is named by more than 8 of them.
All inputs are finite; a program needn't handle non-finite values.
Results may differ from a plain program's by a relative error of at most 0.0013.
Values may be sent and summed in bfloat16 or wider, within the bound.
A program may use at most 128 MiB of HBM per device.

v0:
```python
import functools

import jax
import jax.numpy as jnp
from jax import lax
from jax.experimental import pallas as pl
from jax.experimental.pallas import tpu as pltpu
from jax.sharding import PartitionSpec as P

F32 = jnp.float32
BF16 = jnp.bfloat16
BASE = 256


def iota(shape, axis):
    return lax.broadcasted_iota(jnp.int32, shape, axis)


def nt_dot(a, b):
    return lax.dot_general(a, b, (((1,), (1,)), ((), ())), preferred_element_type=F32)


def spread_kernel(
    devices, capacity, visc_ref, f_ref, w_ref, owner_ref, slot_ref, out_ref, splat_ref, tiles_ref
):
    step = pl.program_id(0)
    group, markers = f_ref.shape
    cells = w_ref.shape[2]
    wide = group * markers
    pick = (iota((markers, wide), 1) % markers == iota((markers, wide), 0)).astype(BF16)
    tiled = jnp.dot(f_ref[...], pick, preferred_element_type=F32)
    block = iota((group, wide), 1) // markers == iota((group, wide), 0)
    forces = jnp.where(block, tiled, 0.0).astype(BF16)
    weights = w_ref[...].reshape(wide, cells)
    tiles = jnp.dot(forces, weights, preferred_element_type=F32).astype(BF16)
    tiles_ref[pl.ds(pl.multiple_of(step * group, group), group), :] = tiles

    @pl.when(step == pl.num_programs(0) - 1)
    def _():
        for x in range(splat_ref.shape[0]):
            splat_ref[x : x + 1, :] = jnp.full((1, 128), visc_ref[x], F32)
        blocks = owner_ref.shape[1]
        rows = devices * capacity
        owner = owner_ref[...]
        matches = (iota((devices, blocks), 0) == owner).astype(F32)
        earlier = (iota((blocks, blocks), 0) < iota((blocks, blocks), 1)).astype(BF16)
        counts = jnp.dot(matches.astype(BF16), earlier, preferred_element_type=F32)
        rank = jnp.sum(counts * matches, axis=0, keepdims=True).astype(jnp.int32)
        target = owner * capacity + rank
        select = (iota((rows, blocks), 0) == target).astype(BF16)
        out = jnp.dot(select, tiles_ref[...], preferred_element_type=F32)
        number = slot_ref[...] + 1
        lane = iota((128, blocks), 0)
        digits = jnp.where(lane == 0, number // BASE, jnp.where(lane == 1, number % BASE, 0))
        meta = nt_dot(select, digits.astype(F32).astype(BF16))
        if capacity % 8 == 0:
            out_ref[:, :, :cells] = out.reshape(devices, capacity, cells).astype(BF16)
            out_ref[:, :, cells:] = meta.reshape(devices, capacity, 128).astype(BF16)
        else:
            for d in range(devices):
                lo, hi = d * capacity, (d + 1) * capacity
                out_ref[d, :, :cells] = out[lo:hi].astype(BF16)
                out_ref[d, :, cells:] = meta[lo:hi].astype(BF16)


def spread(viscosity, forces, weights, owner, slots, devices, capacity):
    blocks, markers, cells = weights.shape
    group = min(blocks, max(8, 256 // markers))
    return pl.pallas_call(
        functools.partial(spread_kernel, devices, capacity),
        out_shape=(
            jax.ShapeDtypeStruct((devices, capacity, cells + 128), BF16),
            jax.ShapeDtypeStruct((viscosity.shape[0], 128), F32),
        ),
        grid=(blocks // group,),
        in_specs=[
            pl.BlockSpec(memory_space=pltpu.SMEM),
            pl.BlockSpec((group, markers), lambda i: (i, 0)),
            pl.BlockSpec((group, markers, cells), lambda i: (i, 0, 0)),
            pl.BlockSpec((1, blocks), lambda i: (0, 0)),
            pl.BlockSpec((1, blocks), lambda i: (0, 0)),
        ],
        out_specs=(
            pl.BlockSpec((devices, capacity, cells + 128), lambda i: (0, 0, 0)),
            pl.BlockSpec((viscosity.shape[0], 128), lambda i: (0, 0)),
        ),
        scratch_shapes=[pltpu.VMEM((blocks, cells), BF16)],
        compiler_params=pltpu.CompilerParams(vmem_limit_bytes=24 << 20),
        cost_estimate=pl.CostEstimate(
            flops=2 * blocks * markers * cells * 64, bytes_accessed=weights.size * 2, transcendentals=0
        ),
    )(viscosity, forces, weights, owner, slots)


def factor(visc):
    inverse, ratio = [], []
    for x in range(len(visc) - 1):
        pivot = 1.0 + 2.0 * visc[x]
        if x:
            pivot = pivot - visc[x] * ratio[-1]
        inverse.append(1.0 / pivot)
        ratio.append(visc[x] * inverse[-1])
    return inverse, ratio


def spikes(inverse, ratio):
    count = len(inverse)
    left = [inverse[0]]
    for x in range(1, count):
        left.append(ratio[x] * left[-1])
    for x in range(count - 2, -1, -1):
        left[x] = left[x] + ratio[x] * left[x + 1]
    right = [inverse[-1]]
    for x in range(count - 2, -1, -1):
        right.append(ratio[x] * right[-1])
    return left, right[::-1]


def put(ends_ref, which, i, value):
    rows = ends_ref.shape[2]
    if rows % 8 == 0:
        start = pl.multiple_of(lax.rem(i * 8, rows), 8)
        ends_ref[i * 8 // rows, which, pl.ds(start, 8), :] = value
    else:
        share = 8 // rows
        for k in range(share):
            ends_ref[i * share + k, which] = value[k * rows : (k + 1) * rows]


def get(ref, i, lane):
    rows = ref.shape[1]
    if rows % 8 == 0:
        start = pl.multiple_of(lax.rem(i * 8, rows), 8)
        return ref[i * 8 // rows, pl.ds(start, 8), lane].astype(F32)
    share = 8 // rows
    parts = [ref[i * share + k, :, lane].astype(F32) for k in range(share)]
    return jnp.concatenate(parts, axis=0)


def local_kernel(visc_ref, velocity_ref, arrived_ref, out_ref, ends_ref, rhs_ref, coef_ref, flat_ref):
    cells_x, rows_y, seg = velocity_ref.shape
    devices, capacity, width = arrived_ref.shape
    rows = devices * capacity
    cells = width - 128
    segments = pl.num_programs(0)
    z = pl.program_id(0)

    @pl.when(z == 0)
    def _():
        visc = [jnp.full((8, seg), visc_ref[x], F32) for x in range(cells_x)]
        inverse, ratio = factor(visc)
        for x in range(cells_x - 1):
            coef_ref[x] = inverse[x]
            coef_ref[cells_x + x] = ratio[x]
        coef_ref[cells_x - 1] = visc[-1]
        if capacity % 8 == 0:
            flat_ref[...] = arrived_ref[...].astype(F32).reshape(rows, width).astype(BF16)
        else:
            parts = [arrived_ref[d].astype(F32) for d in range(devices)]
            flat_ref[...] = jnp.concatenate(parts, axis=0).astype(BF16)

    lane = iota((8, 128), 1)
    base = jnp.where(lane == 0, float(BASE), jnp.where(lane == 1, 1.0, 0.0)).astype(BF16)
    number = nt_dot(base, flat_ref[:, cells:])[0:1, :].astype(jnp.int32) - 1
    place = (iota((rows_y, rows), 0) * segments + z == number).astype(BF16)
    rhs_ref[...] = jnp.dot(place, flat_ref[:, :cells], preferred_element_type=F32)

    def chunk(i, carry):
        at = pl.ds(pl.multiple_of(i * 8, 8), 8)

        def side(x):
            return velocity_ref[x, at, :] + rhs_ref[at, x * seg : (x + 1) * seg]

        values = [side(0) * coef_ref[0]]
        for x in range(1, cells_x - 1):
            values.append(side(x) * coef_ref[x] + coef_ref[cells_x + x] * values[-1])
        last = cells_x - 1
        put(ends_ref, 0, i, side(last) + coef_ref[last] * values[-1])
        value = values[-1]
        out_ref[last - 1, at, :] = value
        for x in range(last - 2, -1, -1):
            value = values[x] + coef_ref[cells_x + x] * value
            out_ref[x, at, :] = value
        put(ends_ref, 1, i, value)
        return carry

    lax.fori_loop(0, rows_y // 8, chunk, 0, unroll=2)


def local_solve(viscosity, velocity, arrived, seg, grid_x):
    cells_x, cells_y, cells_z = velocity.shape
    devices, capacity, width = arrived.shape
    rows = devices * capacity
    return pl.pallas_call(
        local_kernel,
        out_shape=(
            jax.ShapeDtypeStruct((cells_x - 1, cells_y, cells_z), F32),
            jax.ShapeDtypeStruct((grid_x, 2, cells_y // grid_x, cells_z), F32),
        ),
        grid=(cells_z // seg,),
        in_specs=[
            pl.BlockSpec(memory_space=pltpu.SMEM),
            pl.BlockSpec((cells_x, cells_y, seg), lambda i: (0, 0, i)),
            pl.BlockSpec((devices, capacity, width), lambda i: (0, 0, 0)),
        ],
        out_specs=(
            pl.BlockSpec((cells_x - 1, cells_y, seg), lambda i: (0, 0, i)),
            pl.BlockSpec((grid_x, 2, cells_y // grid_x, seg), lambda i: (0, 0, 0, i)),
        ),
        scratch_shapes=[
            pltpu.VMEM((cells_y, cells_x * seg), F32),
            pltpu.VMEM((2 * cells_x, 8, seg), F32),
            pltpu.VMEM((rows, width), BF16),
        ],
        compiler_params=pltpu.CompilerParams(vmem_limit_bytes=24 << 20),
    )(viscosity, velocity, arrived)


def couple(visc_ref, out_ref):
    count, cells_x, lanes = visc_ref.shape
    visc = [visc_ref[:, x, :] for x in range(cells_x)]
    inverse, ratio = factor(visc)
    left, right = spikes(inverse, ratio)
    row = iota((count, lanes), 0)

    def following(value):
        moved = jnp.concatenate([value[1:], value[:1]], axis=0)
        return jnp.where(row == count - 1, 0.0, moved)

    sep, inner, first = visc[-1], visc[-2], visc[0]
    lower = jnp.where(row > 0, -sep * first * left[-1], 0.0)
    center = 1.0 + 2.0 * sep - sep * inner * right[-1] - sep * following(first * left[0])
    upper = -sep * following(inner * right[0])
    previous = jnp.zeros((1, lanes), F32)
    for d in range(count):
        pivot = center[d : d + 1] - lower[d : d + 1] * previous
        inv = 1.0 / pivot
        previous = upper[d : d + 1] * inv
        out_ref[0, d : d + 1, :] = inv
        out_ref[1, d : d + 1, :] = previous
    out_ref[2] = lower
    out_ref[3] = jnp.where(row == count - 1, 0.0, sep)


def reduced(coef_ref, sides_ref, out_ref, step_ref):
    count, _, rows, cells_z = sides_ref.shape
    lanes = coef_ref.shape[2]
    for c in range(cells_z // lanes):
        at = slice(c * lanes, (c + 1) * lanes)
        values = []
        for d in range(count):
            side = sides_ref[d, 0, :, at]
            if d + 1 < count:
                side = side + coef_ref[3, d : d + 1, :] * sides_ref[d + 1, 1, :, at]
            if d:
                side = side - coef_ref[2, d : d + 1, :] * values[-1]
            values.append(side * coef_ref[0, d : d + 1, :])
        value = values[-1]
        out_ref[count - 1, :, at] = value
        for d in range(count - 2, -1, -1):
            before = values[d] - coef_ref[1, d : d + 1, :] * value
            out_ref[d, :, at] = before
            step_ref[d + 1, :, at] = (before - value).astype(BF16)
            value = before
        step_ref[0, :, at] = (-value).astype(BF16)


def partner(me, k, count, sign=1):
    if count & (count - 1):
        return lax.rem(me + count + sign * k, count)
    total, bit = 0, 1
    while bit < count:
        total = total + bit * lax.rem(lax.rem(me // bit, 2) + lax.rem(k // bit, 2), 2)
        bit *= 2
    return total


def greet(count, peer_of):
    barrier = pltpu.get_barrier_semaphore()

    def signal(i, carry):
        pl.semaphore_signal(
            barrier, inc=1, device_id=peer_of(i), device_id_type=pl.DeviceIdType.MESH
        )
        return carry

    lax.fori_loop(1, count, signal, 0)
    pl.semaphore_wait(barrier, count - 1)


def tiles_kernel(count_x, count_y, out_ref, splat_ref, tiles_ref, whole_ref, send, recv, vsend, vrecv, own):
    count = count_x * count_y
    gx, gy = lax.axis_index("gx"), lax.axis_index("gy")
    me = gx * count_y + gy

    def device(i):
        peer = partner(me, i, count)
        return (peer // count_y, lax.rem(peer, count_y))

    def tile_copy(i, slot):
        peer = partner(me, i, count)
        return pltpu.make_async_remote_copy(
            src_ref=out_ref.at[peer],
            dst_ref=tiles_ref.at[slot],
            send_sem=send.at[i],
            recv_sem=recv.at[i],
            device_id=(peer // count_y, lax.rem(peer, count_y)),
            device_id_type=pl.DeviceIdType.MESH,
        )

    def visc_copy(i, slot):
        return pltpu.make_async_remote_copy(
            src_ref=splat_ref,
            dst_ref=whole_ref.at[slot],
            send_sem=vsend.at[i],
            recv_sem=vrecv.at[i],
            device_id=(partner(gx, i, count_x), gy),
            device_id_type=pl.DeviceIdType.MESH,
        )

    own_tile = pltpu.make_async_copy(out_ref.at[me], tiles_ref.at[me], own.at[0])
    own_visc = pltpu.make_async_copy(splat_ref, whole_ref.at[gx], own.at[1])
    own_tile.start()
    own_visc.start()
    greet(count, device)

    def start_tile(i, carry):
        tile_copy(i, me).start()
        return carry

    def start_visc(i, carry):
        visc_copy(i, gx).start()
        return carry

    def finish_tile(i, carry):
        tile_copy(i, partner(me, i, count, -1)).wait()
        return carry

    def finish_visc(i, carry):
        visc_copy(i, partner(gx, i, count_x, -1)).wait()
        return carry

    lax.fori_loop(1, count, start_tile, 0)
    lax.fori_loop(1, count_x, start_visc, 0)
    lax.fori_loop(1, count, finish_tile, 0)
    lax.fori_loop(1, count_x, finish_visc, 0)
    own_tile.wait()
    own_visc.wait()


def exchange_tiles(outgoing, splat, count_x, count_y):
    anywhere = pl.BlockSpec(memory_space=pl.ANY)
    dma = pltpu.SemaphoreType.DMA
    return pl.pallas_call(
        functools.partial(tiles_kernel, count_x, count_y),
        out_shape=(
            jax.ShapeDtypeStruct(outgoing.shape, BF16),
            jax.ShapeDtypeStruct((count_x,) + splat.shape, F32),
        ),
        in_specs=[anywhere, anywhere],
        out_specs=(anywhere, anywhere),
        scratch_shapes=[
            dma((count_x * count_y,)),
            dma((count_x * count_y,)),
            dma((count_x,)),
            dma((count_x,)),
            dma((2,)),
        ],
        compiler_params=pltpu.CompilerParams(
            collective_id=0, has_side_effects=True, vmem_limit_bytes=16 << 20
        ),
    )(outgoing, splat)


def lines_kernel(
    count, ends_ref, whole_ref, out_ref, step_ref,
    sides_ref, solved_ref, steps_ref, coef_ref, send, recv, back, home, back_step, home_step, own
):
    gx, gy = lax.axis_index("gx"), lax.axis_index("gy")

    def device(i):
        return (partner(gx, i, count), gy)

    def copy(source, target, slot, sends, receives, i):
        peer = partner(gx, i, count)
        return pltpu.make_async_remote_copy(
            src_ref=source.at[peer],
            dst_ref=target.at[slot],
            send_sem=sends.at[i],
            recv_sem=receives.at[i],
            device_id=(peer, gy),
            device_id_type=pl.DeviceIdType.MESH,
        )

    def start_all(*groups):
        def start(i, carry):
            for source, target, sends, receives in groups:
                copy(source, target, gx, sends, receives, i).start()
            return carry

        lax.fori_loop(1, count, start, 0)

    def finish_all(*groups):
        def finish(i, carry):
            for source, target, sends, receives in groups:
                copy(source, target, partner(gx, i, count, -1), sends, receives, i).wait()
            return carry

        lax.fori_loop(1, count, finish, 0)

    outward = (ends_ref, sides_ref, send, recv)
    homeward = (
        (solved_ref, out_ref, back, home),
        (steps_ref, step_ref, back_step, home_step),
    )
    greet(count, device)
    start_all(outward)
    mine = pltpu.make_async_copy(ends_ref.at[gx], sides_ref.at[gx], own.at[0])
    mine.start()
    couple(whole_ref, coef_ref)
    mine.wait()
    finish_all(outward)
    reduced(coef_ref, sides_ref, solved_ref, steps_ref)
    kept = pltpu.make_async_copy(solved_ref.at[gx], out_ref.at[gx], own.at[1])
    kept_step = pltpu.make_async_copy(steps_ref.at[gx], step_ref.at[gx], own.at[2])
    kept.start()
    kept_step.start()
    start_all(*homeward)
    kept.wait()
    kept_step.wait()
    finish_all(*homeward)


def exchange_lines(ends, whole):
    count = ends.shape[0]
    single = (count,) + ends.shape[2:]
    dma = pltpu.SemaphoreType.DMA
    return pl.pallas_call(
        functools.partial(lines_kernel, count),
        out_shape=(jax.ShapeDtypeStruct(single, F32), jax.ShapeDtypeStruct(single, BF16)),
        in_specs=[pl.BlockSpec(memory_space=pltpu.VMEM)] * 2,
        out_specs=(pl.BlockSpec(memory_space=pltpu.VMEM),) * 2,
        scratch_shapes=[
            pltpu.VMEM(ends.shape, F32),
            pltpu.VMEM(single, F32),
            pltpu.VMEM(single, BF16),
            pltpu.VMEM((4, count, 128), F32),
            dma((count,)),
            dma((count,)),
            dma((count,)),
            dma((count,)),
            dma((count,)),
            dma((count,)),
            dma((3,)),
        ],
        compiler_params=pltpu.CompilerParams(
            collective_id=1, has_side_effects=True, vmem_limit_bytes=16 << 20
        ),
    )(ends, whole)


def final_kernel(visc_ref, inner_ref, own_ref, step_ref, out_ref, coef_ref):
    count, rows_y, cells_z = inner_ref.shape
    seg = coef_ref.shape[2]

    @pl.when(pl.program_id(0) == 0)
    def _():
        visc = [jnp.full((8, seg), visc_ref[x], F32) for x in range(count + 1)]
        left, right = spikes(*factor(visc))
        for x in range(count):
            coef_ref[x] = visc[0] * left[x]
            coef_ref[count + x] = visc[count - 1] * right[x]

    def chunk(i, carry):
        at = pl.ds(pl.multiple_of(i * 8, 8), 8)
        for c in range(cells_z // seg):
            lane = slice(c * seg, (c + 1) * seg)
            own = get(own_ref, i, lane)
            before = own + get(step_ref, i, lane)
            for x in range(count):
                out_ref[x, at, lane] = (
                    inner_ref[x, at, lane] + coef_ref[x] * before + coef_ref[count + x] * own
                )
            out_ref[count, at, lane] = own
        return carry

    lax.fori_loop(0, rows_y // 8, chunk, 0)


def final(viscosity, inner, own, step, seg):
    count, cells_y, cells_z = inner.shape
    parts = 4
    rows = cells_y // parts
    return pl.pallas_call(
        final_kernel,
        out_shape=jax.ShapeDtypeStruct((count + 1, cells_y, cells_z), F32),
        grid=(parts,),
        in_specs=[
            pl.BlockSpec(memory_space=pltpu.SMEM),
            pl.BlockSpec((count, rows, cells_z), lambda i: (0, i, 0)),
            pl.BlockSpec((own.shape[0] // parts,) + own.shape[1:], lambda i: (i, 0, 0)),
            pl.BlockSpec((own.shape[0] // parts,) + own.shape[1:], lambda i: (i, 0, 0)),
        ],
        out_specs=pl.BlockSpec((count + 1, rows, cells_z), lambda i: (0, i, 0)),
        scratch_shapes=[pltpu.VMEM((2 * count, 8, seg), F32)],
        compiler_params=pltpu.CompilerParams(vmem_limit_bytes=24 << 20),
    )(viscosity, inner, own, step)


def per_device(velocity, viscosity, marker_forces, spread_weights, block_owner, tile_slot):
    cells_x, cells_y, cells_z = velocity.shape
    grid_x = lax.axis_size("gx")
    devices = grid_x * lax.axis_size("gy")
    blocks, _, cells = spread_weights.shape
    capacity = max(2, 2 * blocks // devices)
    seg = cells // cells_x
    outgoing, splat = spread(
        viscosity,
        marker_forces,
        pltpu.with_memory_space_constraint(spread_weights, pltpu.HBM),
        block_owner.reshape(1, blocks),
        tile_slot.reshape(1, blocks),
        devices,
        capacity,
    )
    arrived, whole = exchange_tiles(outgoing, splat, grid_x, devices // grid_x)
    inner, ends = local_solve(viscosity, velocity, arrived, seg, grid_x)
    own, step = exchange_lines(ends, whole)
    return final(viscosity, inner, own, step, seg)


def solution(mesh):
    placed = (
        P("gx", "gy", None),
        P("gx"),
        P(("gx", "gy"), None),
        P(("gx", "gy"), None, None),
        P(("gx", "gy"), None),
        P(("gx", "gy")),
    )
    return jax.shard_map(
        per_device, mesh=mesh, in_specs=placed, out_specs=P("gx", "gy", None), check_vma=False
    )
```

profile of v0, /device:TPU:0, one launch (start us, length us, event | category | flops | bytes accessed | tf_op | source)
XLA Modules:
  0.0 84.8 jit_solution(9249506222475462993)
XLA Ops:
  0.0 0.8 copy.7.f_ref
  0.8 0.0 copy-start.1
  0.8 0.7 copy-done.1
  1.5 0.0 copy-start.2
  1.5 0.7 copy-done.2
  2.1 0.0 copy-start.3
  2.1 0.7 copy-done.3
  2.8 0.0 copy-start
  2.8 7.7 %shard_map.64 = (bf16[32,8,2176]{2,1,0:T(8,128)(2,1)S(1)}, f32[16,128]{1,0:T(8,128)S(1)}) custom-call(f32[16]{0:T(128)S(1)} %copy-done.1, bf16[128,16]{1,0:T(8,128)(2,1)S(1)} %copy.7.f_ref, bf16[128,16,2048]{2,1,0:T(8,128)(2,1)} %w_ref.1, s32[1,128]{1,0:T(1,128)S(1)} %bitcast.2, s32[1,128]{1,0:T(1,128)S(1)} %bitcast.3), custom_call_target="tpu_custom_call" | custom-call | flops 536870912 | bytes 8388608 | tf_op jit(solution)/shard_map/pallas_call | solution.py:69
  10.5 36.8 %shard_map.65 = (bf16[32,8,2176]{2,1,0:T(8,128)(2,1)S(1)}, f32[16,16,128]{2,1,0:T(8,128)S(1)}) custom-call(bf16[32,8,2176]{2,1,0:T(8,128)(2,1)S(1)} %get-tuple-element.13.out_ref, f32[16,128]{1,0:T(8,128)S(1)} %get-tuple-element.14.splat_ref), custom_call_target="tpu_custom_call" | custom-call | tf_op jit(solution)/shard_map/pallas_call | solution.py:354
  47.3 0.0 copy-done
  47.3 5.9 %shard_map.66 = (f32[15,128,512]{2,1,0:T(8,128)S(1)}, f32[16,2,8,512]{3,2,1,0:T(8,128)S(1)}) custom-call(f32[16]{0:T(128)S(1)} %copy-done.1, f32[16,128,512]{2,1,0:T(8,128)S(1)} %copy-done, bf16[32,8,2176]{2,1,0:T(8,128)(2,1)S(1)} %get-tuple-element.15.arrived_ref), custom_call_target="tpu_custom_call" | custom-call | tf_op jit(solution)/shard_map/pallas_call | solution.py:194
  53.2 28.0 %shard_map.67 = (f32[16,8,512]{2,1,0:T(8,128)S(1)}, bf16[16,8,512]{2,1,0:T(8,128)(2,1)S(1)}) custom-call(f32[16,2,8,512]{3,2,1,0:T(8,128)S(1)} %get-tuple-element.17.ends_ref, f32[16,16,128]{2,1,0:T(8,128)S(1)} %get-tuple-element.18.whole_ref), custom_call_target="tpu_custom_call" | custom-call | tf_op jit(solution)/shard_map/pallas_call | solution.py:438
  81.2 3.6 %shard_map.68 = f32[16,128,512]{2,1,0:T(8,128)} custom-call(f32[16]{0:T(128)S(1)} %copy-done.1, f32[15,128,512]{2,1,0:T(8,128)S(1)} %get-tuple-element.16.inner_ref, f32[16,8,512]{2,1,0:T(8,128)S(1)} %get-tuple-element.19.own_ref, bf16[16,8,512]{2,1,0:T(8,128)(2,1)S(1)} %get-tuple-element.20.step_ref), custom_call_target="tpu_custom_call" | custom-call | tf_op jit(solution)/shard_map/pallas_call | solution.py:494
Async XLA Ops:
  0.8 0.7 copy-start.1
  1.5 0.7 copy-start.2
  2.1 0.7 copy-start.3
  2.8 44.5 %copy-start = (f32[16,128,512]{2,1,0:T(8,128)S(1)}, f32[16,128,512]{2,1,0:T(8,128)}, u32[]{:S(2)}) copy-start(f32[16,128,512]{2,1,0:T(8,128)} %velocity_ref.1) | copy-start | bytes 12582916
where the time goes:
time: 85 us; the launch traced here: 84.8 us
  Pallas kernels  81.9 us (96%)
  local copies, waits for them, and re-layouts  2.77 us (3%)
    pallas_call x1, Pallas kernels, exchange_tiles(): pl.pallas_call(functools.partial(tiles_kernel, count_x, count_y), out_sha...  36.8 us
    pallas_call x1, Pallas kernels, exchange_lines(): pl.pallas_call(functools.partial(lines_kernel, count), out_shape=(jax.Sha...  28 us
    pallas_call x1, Pallas kernels, spread(): pl.pallas_call(functools.partial(spread_kernel, devices, capacity), out_s...  7.67 us
    pallas_call x1, Pallas kernels, local_solve(): pl.pallas_call(local_kernel, out_shape=(jax.ShapeDtypeStruct((cells_x - 1...  5.93 us
    pallas_call x1, Pallas kernels, final(): pl.pallas_call(final_kernel, out_shape=jax.ShapeDtypeStruct((count + 1, c...  3.59 us
    unnamed x9, local copies, waits for them, and re-layouts  2.77 us

commit v1 on v0

v1 whole, which is shorter than its diff:
```python
import functools

import jax
import jax.numpy as jnp
from jax import lax
from jax.experimental import pallas as pl
from jax.experimental.pallas import tpu as pltpu
from jax.sharding import PartitionSpec as P

F32 = jnp.float32
BF16 = jnp.bfloat16
BASE = 256
LANES = 128
VISC_LANE = 64
TOP = 32767.0
TINY = 1e-30


def iota(shape, axis):
    return lax.broadcasted_iota(jnp.int32, shape, axis)


def nt_dot(a, b):
    return lax.dot_general(a, b, (((1,), (1,)), ((), ())), preferred_element_type=F32)


def tn_dot(a, b):
    return lax.dot_general(a, b, (((0,), (0,)), ((), ())), preferred_element_type=F32)


def factor(visc):
    inverse, ratio = [], []
    for x in range(len(visc) - 1):
        pivot = 1.0 + 2.0 * visc[x]
        if x:
            pivot = pivot - visc[x] * ratio[-1]
        inverse.append(1.0 / pivot)
        ratio.append(visc[x] * inverse[-1])
    return inverse, ratio


def spikes(inverse, ratio):
    count = len(inverse)
    left = [inverse[0]]
    for x in range(1, count):
        left.append(ratio[x] * left[-1])
    for x in range(count - 2, -1, -1):
        left[x] = left[x] + ratio[x] * left[x + 1]
    right = [inverse[-1]]
    for x in range(count - 2, -1, -1):
        right.append(ratio[x] * right[-1])
    return left, right[::-1]


def end_weights(visc, inverse, ratio):
    count = len(inverse)
    last, run = [], visc[-1]
    for x in range(count - 1, -1, -1):
        last.append(run * inverse[x])
        run = run * ratio[x]
    reach = [jnp.ones_like(inverse[0])]
    for x in range(count - 1):
        reach.append(reach[-1] * ratio[x])
    first, total = [], None
    for x in range(count - 1, -1, -1):
        total = reach[x] if total is None else reach[x] + ratio[x + 1] * total
        first.append(visc[0] * inverse[x] * total)
    return last[::-1], first[::-1]


def couple(visc, stride, out_ref):
    rows, lanes = visc[0].shape
    count = rows // stride
    inverse, ratio = factor(visc)
    left, right = spikes(inverse, ratio)
    row = iota((rows, lanes), 0)

    def following(value):
        moved = jnp.concatenate([value[stride:], value[:stride]], axis=0)
        return jnp.where(row >= rows - stride, 0.0, moved)

    sep, inner, first = visc[-1], visc[-2], visc[0]
    lower = jnp.where(row >= stride, -sep * first * left[-1], 0.0)
    center = 1.0 + 2.0 * sep - sep * inner * right[-1] - sep * following(first * left[0])
    upper = -sep * following(inner * right[0])
    final_rows = row >= rows - stride
    held = jnp.where(final_rows, 0.0, sep / jnp.where(final_rows, 1.0, following(first)))
    previous = jnp.zeros((1, lanes), F32)
    for d in range(count):
        at = slice(d * stride, d * stride + 1)
        pivot = center[at] - lower[at] * previous
        inv = 1.0 / pivot
        previous = upper[at] * inv
        out_ref[0, d : d + 1, :] = inv
        out_ref[1, d : d + 1, :] = previous
        out_ref[2, d : d + 1, :] = lower[at]
        out_ref[3, d : d + 1, :] = held[at]


def partner(me, k, count, sign=1):
    if count & (count - 1):
        return lax.rem(me + count + sign * k, count)
    total, bit = 0, 1
    while bit < count:
        total = total + bit * lax.rem(lax.rem(me // bit, 2) + lax.rem(k // bit, 2), 2)
        bit *= 2
    return total


def peak(values):
    most = jnp.abs(values[0])
    for value in values[1:]:
        most = jnp.maximum(most, jnp.abs(value))
    return jnp.maximum(jnp.max(most, axis=0, keepdims=True), TINY)


def pack(high, low, inverse):
    high = jnp.round(high * inverse).astype(jnp.int32)
    low = jnp.round(low * inverse).astype(jnp.int32)
    return high * 65536 + low


def unpack(code, scale):
    low = (code << 16) >> 16
    high = (code - low) >> 16
    return high.astype(F32) * scale, low.astype(F32) * scale


def step_kernel(
    count_x, count_y, capacity, chunks,
    visc_hbm, forces_hbm, weights_hbm, owner_hbm, slot_hbm, velocity_hbm,
    inner_ref, back_ref, back_scale_ref, mix_ref,
    visc_ref, forces_ref, owner_ref, slot_ref, weights_ref, velocity_ref,
    spread_ref, outgoing_ref, tiles_ref, meta_ref, metas_ref, place_ref, tile_ends_ref, ends_ref,
    local_ref, weight_ref, couple_ref, code_ref, code_scale_ref, sides_ref, sides_scale_ref,
    solved_ref, home_ref, home_scale_ref, rhs_ref, flat_ref,
    own, wsem, tile_send, tile_recv, meta_send, meta_recv,
    code_send, code_recv, cscale_send, cscale_recv, home_send, home_recv, hscale_send, hscale_recv,
):
    devices = count_x * count_y
    cells_x, rows_y, cells_z = velocity_ref.shape
    markers, blocks = forces_ref.shape
    cells = outgoing_ref.shape[2]
    wide = blocks * markers
    rows = devices * capacity
    share = code_ref.shape[1]
    width = cells // chunks
    segments = cells_z // LANES
    last = cells_x - 1
    gx, gy = lax.axis_index("gx"), lax.axis_index("gy")
    me = gx * count_y + gy

    def device(i):
        peer = partner(me, i, devices)
        return (peer // count_y, lax.rem(peer, count_y))

    def loop(first, end, body, unroll=1):
        def step(i, carry):
            body(i)
            return carry

        lax.fori_loop(first, end, step, 0, unroll=unroll)

    barrier = pltpu.get_barrier_semaphore()

    def greet(i):
        pl.semaphore_signal(
            barrier, inc=1, device_id=device(i), device_id_type=pl.DeviceIdType.MESH
        )

    small = [
        pltpu.make_async_copy(source, target, own.at[k])
        for k, (source, target) in enumerate(
            ((owner_hbm, owner_ref), (forces_hbm, forces_ref), (slot_hbm, slot_ref), (visc_hbm, visc_ref))
        )
    ]
    for copy in small:
        copy.start()

    def weight_copy(c):
        at = pl.ds(pl.multiple_of(c * width, width), width)
        return pltpu.make_async_copy(weights_hbm.at[:, :, at], weights_ref.at[c], wsem.at[c])

    loop(0, chunks, lambda c: weight_copy(c).start())
    velocity_copy = pltpu.make_async_copy(velocity_hbm, velocity_ref, own.at[4])
    velocity_copy.start()
    loop(1, devices, greet)
    for copy in small:
        copy.wait()

    owner = owner_ref[...]
    matches = (iota((devices, blocks), 0) == owner).astype(BF16)
    earlier = (iota((blocks, blocks), 0) < iota((blocks, blocks), 1)).astype(BF16)
    counts = jnp.dot(matches, earlier, preferred_element_type=F32)
    rank = jnp.sum(counts * matches.astype(F32), axis=0, keepdims=True).astype(jnp.int32)
    target = owner * capacity + rank
    select = (iota((rows, blocks), 0) == target).astype(BF16)
    choose = (iota((markers, wide), 1) % markers == iota((markers, wide), 0)).astype(BF16)
    tiled = tn_dot(forces_ref[...], choose)
    offset = iota((blocks, wide), 1) - iota((blocks, wide), 0) * markers
    spread = jnp.where((offset >= 0) & (offset < markers), tiled, 0.0).astype(BF16)
    spread_ref[...] = jnp.dot(select, spread, preferred_element_type=F32).astype(BF16)

    number = slot_ref[...] + 1
    high = number // BASE
    ranked = iota((LANES, blocks), 0) == rank
    digits = [jnp.where(ranked, d, 0).astype(F32).astype(BF16) for d in (high, number - high * BASE)]
    meta = nt_dot(matches, digits[0]) * BASE + nt_dot(matches, digits[1])
    lane = iota((1, LANES), 1)
    viscous = jnp.zeros((1, LANES), F32)
    for x in range(cells_x):
        viscous = jnp.where(lane == VISC_LANE + x, visc_ref[x], viscous)
    meta = meta + viscous
    for d in range(devices):
        meta_ref[d] = meta[d : d + 1]

    def spread_chunk(c):
        weight_copy(c).wait()
        at = pl.ds(pl.multiple_of(c * width, width), width)
        out = jnp.dot(
            spread_ref[...], weights_ref[c].reshape(wide, width), preferred_element_type=F32
        )
        if capacity % 8 == 0:
            outgoing_ref[:, :, at] = out.reshape(devices, capacity, width).astype(BF16)
        else:
            for d in range(devices):
                outgoing_ref[d, :, at] = out[d * capacity : (d + 1) * capacity].astype(BF16)

    loop(0, chunks, spread_chunk)

    def remote(source, target, sends, receives, i, peer):
        return pltpu.make_async_remote_copy(
            src_ref=source,
            dst_ref=target,
            send_sem=sends.at[i],
            recv_sem=receives.at[i],
            device_id=peer,
            device_id_type=pl.DeviceIdType.MESH,
        )

    def tile_copy(i, slot):
        peer = partner(me, i, devices)
        return remote(outgoing_ref.at[peer], tiles_ref.at[slot], tile_send, tile_recv, i, device(i))

    def meta_copy(i, slot):
        peer = partner(me, i, devices)
        return remote(meta_ref.at[peer], metas_ref.at[slot], meta_send, meta_recv, i, device(i))

    def came(i):
        return partner(me, i, devices, -1)

    pl.semaphore_wait(barrier, devices - 1)
    loop(1, devices, lambda i: meta_copy(i, me).start())
    loop(1, devices, lambda i: tile_copy(i, me).start())
    tiles_ref[me] = outgoing_ref[me]
    metas_ref[me] = meta_ref[me]

    visc = [jnp.full((8, LANES), visc_ref[x], F32) for x in range(cells_x)]
    inverse, ratio = factor(visc)
    for x in range(last):
        local_ref[x] = inverse[x]
        local_ref[cells_x + x] = ratio[x]
    to_last, to_first = end_weights(visc, inverse, ratio)
    for x in range(last):
        weight_ref[x] = to_last[x]
        weight_ref[cells_x + x] = to_first[x]
    left, right = spikes(inverse, ratio)
    for x in range(last):
        mix_ref[x] = visc[0] * left[x]
        mix_ref[last + x] = visc[last - 1] * right[x]

    def ends_of(side):
        value = side(0)
        high, low = value * weight_ref[0], value * weight_ref[cells_x]
        for x in range(1, last):
            value = side(x)
            high = high + value * weight_ref[x]
            low = low + value * weight_ref[cells_x + x]
        return high + side(last), low

    velocity_copy.wait()

    def velocity_ends(i):
        at = pl.ds(pl.multiple_of(i * 8, 8), 8)
        for s in range(segments):
            lanes = slice(s * LANES, (s + 1) * LANES)
            high, low = ends_of(lambda x: velocity_ref[x, at, lanes])
            ends_ref[0, at, lanes] = high
            ends_ref[1, at, lanes] = low

    loop(0, rows_y // 8, velocity_ends)

    loop(1, devices, lambda i: meta_copy(i, came(i)).wait())
    metas = jnp.concatenate([metas_ref[d] for d in range(devices)], axis=0)
    couple(
        [
            jnp.broadcast_to(metas[:, VISC_LANE + x : VISC_LANE + x + 1], (devices, LANES))
            for x in range(cells_x)
        ],
        count_y,
        couple_ref,
    )
    lane = iota((devices, LANES), 1)
    numbers = jnp.where(lane < capacity, metas, 0.0).astype(jnp.int32)
    high = numbers // BASE
    expand = (iota((LANES, rows), 1) % capacity == iota((LANES, rows), 0)).astype(BF16)
    number = jnp.zeros((devices, rows), F32)
    for digit, base in ((high, float(BASE)), (numbers - high * BASE, 1.0)):
        number = number + base * jnp.dot(
            digit.astype(F32).astype(BF16), expand, preferred_element_type=F32
        )
    offset = iota((devices, rows), 1) - iota((devices, rows), 0) * capacity
    number = jnp.where((offset >= 0) & (offset < capacity), number, 0.0)
    number = jnp.sum(number, axis=0, keepdims=True).astype(jnp.int32) - 1
    for s in range(segments):
        place_ref[s] = (iota((rows_y, rows), 0) * segments + s == number).astype(BF16)

    def tile_ends(slot):
        at = pl.ds(pl.multiple_of(slot * capacity, capacity), capacity)
        high, low = ends_of(lambda x: tiles_ref[slot, :, x * LANES : (x + 1) * LANES].astype(F32))
        tile_ends_ref[at, :LANES] = high
        tile_ends_ref[at, LANES:] = low

    def flatten():
        if capacity % 8 == 0:
            flat_ref[...] = tiles_ref[...].astype(F32).reshape(rows, cells).astype(BF16)
        else:
            parts = [tiles_ref[d].astype(F32) for d in range(devices)]
            flat_ref[...] = jnp.concatenate(parts, axis=0).astype(BF16)

    if capacity % 8 == 0:
        tile_ends(me)

        def arrive(i):
            tile_copy(i, came(i)).wait_recv()
            tile_ends(came(i))

        loop(1, devices, arrive)
    else:
        loop(1, devices, lambda i: tile_copy(i, came(i)).wait_recv())
        flatten()

        def flat_ends(i):
            at = pl.ds(pl.multiple_of(i * 8, 8), 8)
            high, low = ends_of(lambda x: flat_ref[at, x * LANES : (x + 1) * LANES].astype(F32))
            tile_ends_ref[at, :LANES] = high
            tile_ends_ref[at, LANES:] = low

        loop(0, rows // 8, flat_ends)

    found = tile_ends_ref[...]
    coarse = found.astype(BF16)
    fine = (found - coarse.astype(F32)).astype(BF16)
    for s in range(segments):
        lanes = slice(s * LANES, (s + 1) * LANES)
        placed = jnp.dot(place_ref[s], coarse, preferred_element_type=F32)
        placed = placed + jnp.dot(place_ref[s], fine, preferred_element_type=F32)
        ends_ref[0, :, lanes] = ends_ref[0, :, lanes] + placed[:, :LANES]
        ends_ref[1, :, lanes] = ends_ref[1, :, lanes] + placed[:, LANES:]

    def line_copy(source, target, sends, receives, i, slot):
        peer = partner(gx, i, count_x)
        return remote(source.at[peer], target.at[slot], sends, receives, i, (peer, gy))

    outward = ((code_ref, sides_ref, code_send, code_recv), (code_scale_ref, sides_scale_ref, cscale_send, cscale_recv))
    homeward = ((home_ref, back_ref, home_send, home_recv), (home_scale_ref, back_scale_ref, hscale_send, hscale_recv))

    def start(groups, i):
        for group in groups:
            line_copy(*group, i, gx).start()

    def finish(groups, i):
        for group in groups:
            line_copy(*group, i, partner(gx, i, count_x, -1)).wait()

    def code_rows(i):
        at = pl.ds(pl.multiple_of(i * 8, 8), 8)
        pairs = []
        for s in range(segments):
            lanes = slice(s * LANES, (s + 1) * LANES)
            pairs.append((ends_ref[0, at, lanes], ends_ref[1, at, lanes]))
        most = peak([value for pair in pairs for value in pair])
        inverse = TOP / most
        codes = [pack(high, low, inverse) for high, low in pairs]
        scale = most * (1.0 / TOP)
        return codes, scale

    if share % 8 == 0:

        def code_peer(peer):
            most = None
            for k in range(share // 8):
                at = pl.ds(pl.multiple_of(peer * share + k * 8, 8), 8)
                top = peak([ends_ref[w, at, s * LANES : (s + 1) * LANES] for s in range(segments) for w in (0, 1)])
                most = top if most is None else jnp.maximum(most, top)
            inverse = TOP / most
            code_scale_ref[peer] = most * (1.0 / TOP)
            for k in range(share // 8):
                at = pl.ds(pl.multiple_of(peer * share + k * 8, 8), 8)
                for s in range(segments):
                    lanes = slice(s * LANES, (s + 1) * LANES)
                    code_ref[peer, k * 8 : (k + 1) * 8, lanes] = pack(
                        ends_ref[0, at, lanes], ends_ref[1, at, lanes], inverse
                    )

        def code_and_start(i):
            code_peer(partner(gx, i, count_x))
            start(outward, i)

        loop(1, count_x, code_and_start)
        code_peer(gx)
    else:
        group = 8 // share
        for i in range(rows_y // 8):
            codes, scale = code_rows(i)
            for k in range(group):
                code_scale_ref[i * group + k] = scale
                for s in range(segments):
                    code_ref[i * group + k, :, s * LANES : (s + 1) * LANES] = codes[s][k * share : (k + 1) * share]
        loop(1, count_x, lambda i: start(outward, i))
    sides_ref[gx] = code_ref[gx]
    sides_scale_ref[gx] = code_scale_ref[gx]

    if capacity % 8 == 0:
        flatten()
    for s in range(segments):
        lanes = slice(s * LANES, (s + 1) * LANES)
        rhs_ref[...] = jnp.dot(place_ref[s], flat_ref[:, : last * LANES], preferred_element_type=F32)

        def solve(i):
            at = pl.ds(pl.multiple_of(i * 8, 8), 8)
            values = []
            for x in range(last):
                side = velocity_ref[x, at, lanes] + rhs_ref[at, x * LANES : (x + 1) * LANES]
                side = side * local_ref[x]
                values.append(side + local_ref[cells_x + x] * values[-1] if x else side)
            value = values[-1]
            inner_ref[last - 1, at, lanes] = value
            for x in range(last - 2, -1, -1):
                value = values[x] + local_ref[cells_x + x] * value
                inner_ref[x, at, lanes] = value

        loop(0, rows_y // 8, solve, unroll=2)

    loop(1, count_x, lambda i: finish(outward, i))

    most = jnp.full((share, LANES), 0.0, F32)
    for s in range(segments):
        lanes = slice(s * LANES, (s + 1) * LANES)
        values = []
        after = None
        sides = [unpack(sides_ref[d, :, lanes], sides_scale_ref[d]) for d in range(count_x)]
        for d in range(count_x):
            side = sides[d][0]
            if d + 1 < count_x:
                side = side + couple_ref[3, d : d + 1, :] * sides[d + 1][1]
            if d:
                side = side - couple_ref[2, d : d + 1, :] * values[-1]
            values.append(side * couple_ref[0, d : d + 1, :])
        value = values[-1]
        solved_ref[count_x - 1, :, lanes] = value
        most = jnp.maximum(most, jnp.abs(value))
        for d in range(count_x - 2, -1, -1):
            value = values[d] - couple_ref[1, d : d + 1, :] * value
            solved_ref[d, :, lanes] = value
            most = jnp.maximum(most, jnp.abs(value))

    most = jnp.maximum(jnp.max(most, axis=0, keepdims=True), TINY)
    inverse = TOP / most
    scale = most * (1.0 / TOP)

    def home_code(d):
        home_scale_ref[d] = scale
        before = jnp.where(d > 0, 1.0, 0.0)
        for s in range(segments):
            lanes = slice(s * LANES, (s + 1) * LANES)
            home_ref[d, :, lanes] = pack(
                solved_ref[d, :, lanes], solved_ref[jnp.maximum(d - 1, 0), :, lanes] * before, inverse
            )

    def home_and_start(i):
        home_code(partner(gx, i, count_x))
        start(homeward, i)

    loop(1, count_x, home_and_start)
    home_code(gx)
    back_ref[gx] = home_ref[gx]
    back_scale_ref[gx] = home_scale_ref[gx]
    loop(1, devices, lambda i: tile_copy(i, came(i)).wait_send())
    loop(1, count_x, lambda i: finish(homeward, i))


def step(viscosity, forces, weights, owner, slots, velocity, grid_x, grid_y, capacity):
    cells_x, cells_y, cells_z = velocity.shape
    blocks, markers, cells = weights.shape
    devices = grid_x * grid_y
    rows = devices * capacity
    share = cells_y // grid_x
    chunks = 4
    dma = pltpu.SemaphoreType.DMA
    vmem = pltpu.VMEM
    anywhere = pl.BlockSpec(memory_space=pl.ANY)
    whole = pl.BlockSpec(memory_space=pltpu.VMEM)
    line = (grid_x, share, cells_z)
    line_scale = (grid_x, 1, LANES)

    def keep(value):
        return pltpu.with_memory_space_constraint(value, pltpu.HBM)

    return pl.pallas_call(
        functools.partial(step_kernel, grid_x, grid_y, capacity, chunks),
        out_shape=(
            jax.ShapeDtypeStruct((cells_x - 1, cells_y, cells_z), F32),
            jax.ShapeDtypeStruct(line, jnp.int32),
            jax.ShapeDtypeStruct(line_scale, F32),
            jax.ShapeDtypeStruct((2 * (cells_x - 1), 8, LANES), F32),
        ),
        in_specs=[anywhere] * 6,
        out_specs=(whole,) * 4,
        scratch_shapes=[
            pltpu.SMEM((cells_x,), F32),
            vmem((markers, blocks), BF16),
            vmem((1, blocks), jnp.int32),
            vmem((1, blocks), jnp.int32),
            vmem((chunks, blocks, markers, cells // chunks), BF16),
            vmem((cells_x, cells_y, cells_z), F32),
            vmem((rows, blocks * markers), BF16),
            vmem((devices, capacity, cells), BF16),
            vmem((devices, capacity, cells), BF16),
            vmem((devices, 1, LANES), F32),
            vmem((devices, 1, LANES), F32),
            vmem((cells_z // LANES, cells_y, rows), BF16),
            vmem((rows, 2 * LANES), F32),
            vmem((2, cells_y, cells_z), F32),
            vmem((2 * cells_x, 8, LANES), F32),
            vmem((2 * cells_x, 8, LANES), F32),
            vmem((4, grid_x, LANES), F32),
            vmem(line, jnp.int32),
            vmem(line_scale, F32),
            vmem(line, jnp.int32),
            vmem(line_scale, F32),
            vmem(line, F32),
            vmem(line, jnp.int32),
            vmem(line_scale, F32),
            vmem((cells_y, (cells_x - 1) * LANES), F32),
            vmem((rows, cells), BF16),
            dma((5,)),
            dma((chunks,)),
            dma((devices,)),
            dma((devices,)),
            dma((devices,)),
            dma((devices,)),
        ]
        + [dma((grid_x,))] * 8,
        compiler_params=pltpu.CompilerParams(
            collective_id=0, has_side_effects=True, vmem_limit_bytes=40 << 20
        ),
    )(
        keep(viscosity), keep(forces), keep(weights), keep(owner), keep(slots), keep(velocity)
    )


def rows_of(ref, i):
    rows = ref.shape[1]
    if rows % 8 == 0:
        start = pl.multiple_of(lax.rem(i * 8, rows), 8)
        return lambda lane: ref[i * 8 // rows, pl.ds(start, 8), lane]
    share = 8 // rows
    return lambda lane: jnp.concatenate([ref[i * share + k, :, lane] for k in range(share)], axis=0)


def scale_of(ref, i, rows):
    if rows % 8 == 0:
        return ref[i * 8 // rows]
    share = 8 // rows
    parts = [jnp.broadcast_to(ref[i * share + k], (rows, LANES)) for k in range(share)]
    return jnp.concatenate(parts, axis=0)


def final_kernel(inner_ref, back_ref, scale_ref, mix_ref, out_ref):
    count, rows_y, cells_z = inner_ref.shape

    def chunk(i, carry):
        at = pl.ds(pl.multiple_of(i * 8, 8), 8)
        codes = rows_of(back_ref, i)
        scale = scale_of(scale_ref, i, back_ref.shape[1])
        for c in range(cells_z // LANES):
            lane = slice(c * LANES, (c + 1) * LANES)
            last, before = unpack(codes(lane), scale)
            for x in range(count):
                out_ref[x, at, lane] = (
                    inner_ref[x, at, lane] + mix_ref[x] * before + mix_ref[count + x] * last
                )
            out_ref[count, at, lane] = last
        return carry

    lax.fori_loop(0, rows_y // 8, chunk, 0)


def final(inner, back, scale, mix):
    count, cells_y, cells_z = inner.shape
    parts = 4
    rows = cells_y // parts
    peers = back.shape[0] // parts
    return pl.pallas_call(
        final_kernel,
        out_shape=jax.ShapeDtypeStruct((count + 1, cells_y, cells_z), F32),
        grid=(parts,),
        in_specs=[
            pl.BlockSpec((count, rows, cells_z), lambda i: (0, i, 0)),
            pl.BlockSpec((peers,) + back.shape[1:], lambda i: (i, 0, 0)),
            pl.BlockSpec((peers,) + scale.shape[1:], lambda i: (i, 0, 0)),
            pl.BlockSpec(mix.shape, lambda i: (0, 0, 0)),
        ],
        out_specs=pl.BlockSpec((count + 1, rows, cells_z), lambda i: (0, i, 0)),
        compiler_params=pltpu.CompilerParams(vmem_limit_bytes=24 << 20),
    )(inner, back, scale, mix)


def per_device(velocity, viscosity, marker_forces, spread_weights, block_owner, tile_slot):
    grid_x, grid_y = lax.axis_size("gx"), lax.axis_size("gy")
    blocks = spread_weights.shape[0]
    capacity = max(2, 2 * blocks // (grid_x * grid_y))
    inner, back, scale, mix = step(
        viscosity,
        marker_forces.T,
        spread_weights,
        block_owner.reshape(1, blocks),
        tile_slot.reshape(1, blocks),
        velocity,
        grid_x,
        grid_y,
        capacity,
    )
    return final(inner, back, scale, mix)


def solution(mesh):
    placed = (
        P("gx", "gy", None),
        P("gx"),
        P(("gx", "gy"), None),
        P(("gx", "gy"), None, None),
        P(("gx", "gy"), None),
        P(("gx", "gy")),
    )
    return jax.shard_map(
        per_device, mesh=mesh, in_specs=placed, out_specs=P("gx", "gy", None), check_vma=False
    )
```

time: 85 us -> 58 us (0.68)
  Pallas kernels: 81.9 us -> 57.9 us
  local copies, waits for them, and re-layouts: 2.77 us -> 0 us
    pallas_call x4 -> x1, Pallas kernels: 78.4 us -> 54.9 us  [step(): pl.pallas_call(functools.partial(step_kernel, grid_x, grid_y, capacity, c...]
    unnamed x9 -> x0, local copies, waits for them, and re-layouts: 2.77 us -> none
where the time goes in v1:
time: 58 us; the launch traced here: 57.9 us
  Pallas kernels  57.9 us (100%)
    pallas_call x1, Pallas kernels, step(): pl.pallas_call(functools.partial(step_kernel, grid_x, grid_y, capacity, c...  54.9 us
    pallas_call x1, Pallas kernels, final(): pl.pallas_call(final_kernel, out_shape=jax.ShapeDtypeStruct((count + 1, c...  2.97 us

profile of v1, /device:TPU:0, one launch (start us, length us, event | category | flops | bytes accessed | tf_op | source)
XLA Modules:
  0.0 57.9 jit_solution(1164283614225102591)
XLA Ops:
  0.0 54.9 %shard_map.64 = (f32[15,128,512]{2,1,0:T(8,128)S(1)}, s32[16,8,512]{2,1,0:T(8,128)S(1)}, f32[16,1,128]{2,1,0:T(1,128)S(1)}, f32[30,8,128]{2,1,0:T(8,128)S(1)}) custom-call(f32[16]{0:T(128)} %visc_hbm.1, bf16[16,128]{1,0:T(8,128)(2,1)} %bitcast.3, bf16[128,16,2048]{2,1,0:T(8,128)(2,1)} %weights_hbm.1, s32[1,128]{1,0:T(1,128)} %bitcast.4, s32[1,128]{1,0:T(1,128)} %bitcast.5, ...), custom_call_target="tpu_custom_call" | custom-call | tf_op jit(solution)/shard_map/pallas_call | solution.py:510
  54.9 3.0 %shard_map.65 = f32[16,128,512]{2,1,0:T(8,128)} custom-call(f32[15,128,512]{2,1,0:T(8,128)S(1)} %get-tuple-element.9.inner_ref, s32[16,8,512]{2,1,0:T(8,128)S(1)} %get-tuple-element.10.back_ref, f32[16,1,128]{2,1,0:T(1,128)S(1)} %get-tuple-element.11.scale_ref, f32[30,8,128]{2,1,0:T(8,128)S(1)} %get-tuple-element.12.mix_ref), custom_call_target="tpu_custom_call" | custom-call | tf_op jit(solution)/shard_map/pallas_call | solution.py:605

commit v2 on v1

--- a/solution.py
+++ b/solution.py
@@ -97,14 +97,22 @@
         out_ref[3, d : d + 1, :] = held[at]
 
 
-def partner(me, k, count, sign=1):
+def peers(me, count):
     if count & (count - 1):
-        return lax.rem(me + count + sign * k, count)
-    total, bit = 0, 1
+        return (lambda k: lax.rem(me + k, count)), (lambda k: lax.rem(me + count - k, count))
+    steps, bit = [], 1
     while bit < count:
-        total = total + bit * lax.rem(lax.rem(me // bit, 2) + lax.rem(k // bit, 2), 2)
+        steps.append(bit - 2 * bit * lax.rem(me // bit, 2))
         bit *= 2
-    return total
+
+    def peer(k):
+        moved = me
+        for n, step in enumerate(steps):
+            if k >> n & 1:
+                moved = moved + step
+        return moved
+
+    return peer, peer
 
 
 def peak(values):
@@ -150,9 +158,18 @@
     gx, gy = lax.axis_index("gx"), lax.axis_index("gy")
     me = gx * count_y + gy
 
+    to_x, from_x = peers(gx, count_x)
+    to_y, from_y = peers(gy, count_y)
+
     def device(i):
-        peer = partner(me, i, devices)
-        return (peer // count_y, lax.rem(peer, count_y))
+        return (to_x(i // count_y), to_y(i % count_y))
+
+    def index(i):
+        px, py = device(i)
+        return px * count_y + py
+
+    def came(i):
+        return from_x(i // count_y) * count_y + from_y(i % count_y)
 
     def loop(first, end, body, unroll=1):
         def step(i, carry):
@@ -163,7 +180,7 @@
 
     barrier = pltpu.get_barrier_semaphore()
 
-    def greet(i):
+    for i in range(1, devices):
         pl.semaphore_signal(
             barrier, inc=1, device_id=device(i), device_id_type=pl.DeviceIdType.MESH
         )
@@ -184,7 +201,6 @@
     loop(0, chunks, lambda c: weight_copy(c).start())
     velocity_copy = pltpu.make_async_copy(velocity_hbm, velocity_ref, own.at[4])
     velocity_copy.start()
-    loop(1, devices, greet)
     for copy in small:
         copy.wait()
 
@@ -239,19 +255,18 @@
         )
 
     def tile_copy(i, slot):
-        peer = partner(me, i, devices)
+        peer = index(i)
         return remote(outgoing_ref.at[peer], tiles_ref.at[slot], tile_send, tile_recv, i, device(i))
 
     def meta_copy(i, slot):
-        peer = partner(me, i, devices)
+        peer = index(i)
         return remote(meta_ref.at[peer], metas_ref.at[slot], meta_send, meta_recv, i, device(i))
 
-    def came(i):
-        return partner(me, i, devices, -1)
-
     pl.semaphore_wait(barrier, devices - 1)
-    loop(1, devices, lambda i: meta_copy(i, me).start())
-    loop(1, devices, lambda i: tile_copy(i, me).start())
+    for i in range(1, devices):
+        meta_copy(i, me).start()
+    for i in range(1, devices):
+        tile_copy(i, me).start()
     tiles_ref[me] = outgoing_ref[me]
     metas_ref[me] = meta_ref[me]
 
@@ -290,7 +305,8 @@
 
     loop(0, rows_y // 8, velocity_ends)
 
-    loop(1, devices, lambda i: meta_copy(i, came(i)).wait())
+    for i in range(1, devices):
+        meta_copy(i, came(i)).wait()
     metas = jnp.concatenate([metas_ref[d] for d in range(devices)], axis=0)
     couple(
         [
@@ -313,7 +329,9 @@
     number = jnp.where((offset >= 0) & (offset < capacity), number, 0.0)
     number = jnp.sum(number, axis=0, keepdims=True).astype(jnp.int32) - 1
     for s in range(segments):
-        place_ref[s] = (iota((rows_y, rows), 0) * segments + s == number).astype(BF16)
+        place_ref[s * rows_y : (s + 1) * rows_y] = (
+            iota((rows_y, rows), 0) * segments + s == number
+        ).astype(BF16)
 
     def tile_ends(slot):
         at = pl.ds(pl.multiple_of(slot * capacity, capacity), capacity)
@@ -331,13 +349,12 @@
     if capacity % 8 == 0:
         tile_ends(me)
 
-        def arrive(i):
+        for i in range(1, devices):
             tile_copy(i, came(i)).wait_recv()
             tile_ends(came(i))
-
-        loop(1, devices, arrive)
     else:
-        loop(1, devices, lambda i: tile_copy(i, came(i)).wait_recv())
+        for i in range(1, devices):
+            tile_copy(i, came(i)).wait_recv()
         flatten()
 
         def flat_ends(i):
@@ -351,15 +368,18 @@
     found = tile_ends_ref[...]
     coarse = found.astype(BF16)
     fine = (found - coarse.astype(F32)).astype(BF16)
+    both = jnp.concatenate([coarse, fine], axis=1)
+    placed = jnp.dot(place_ref[...], both, preferred_element_type=F32)
     for s in range(segments):
         lanes = slice(s * LANES, (s + 1) * LANES)
-        placed = jnp.dot(place_ref[s], coarse, preferred_element_type=F32)
-        placed = placed + jnp.dot(place_ref[s], fine, preferred_element_type=F32)
-        ends_ref[0, :, lanes] = ends_ref[0, :, lanes] + placed[:, :LANES]
-        ends_ref[1, :, lanes] = ends_ref[1, :, lanes] + placed[:, LANES:]
+        part = placed[s * rows_y : (s + 1) * rows_y]
+        for w in (0, 1):
+            ends_ref[w, :, lanes] = ends_ref[w, :, lanes] + (
+                part[:, w * LANES : (w + 1) * LANES] + part[:, (w + 2) * LANES : (w + 3) * LANES]
+            )
 
     def line_copy(source, target, sends, receives, i, slot):
-        peer = partner(gx, i, count_x)
+        peer = to_x(i)
         return remote(source.at[peer], target.at[slot], sends, receives, i, (peer, gy))
 
     outward = ((code_ref, sides_ref, code_send, code_recv), (code_scale_ref, sides_scale_ref, cscale_send, cscale_recv))
@@ -371,7 +391,7 @@
 
     def finish(groups, i):
         for group in groups:
-            line_copy(*group, i, partner(gx, i, count_x, -1)).wait()
+            line_copy(*group, i, from_x(i)).wait()
 
     def code_rows(i):
         at = pl.ds(pl.multiple_of(i * 8, 8), 8)
@@ -403,11 +423,9 @@
                         ends_ref[0, at, lanes], ends_ref[1, at, lanes], inverse
                     )
 
-        def code_and_start(i):
-            code_peer(partner(gx, i, count_x))
+        for i in range(1, count_x):
+            code_peer(to_x(i))
             start(outward, i)
-
-        loop(1, count_x, code_and_start)
         code_peer(gx)
     else:
         group = 8 // share
@@ -417,7 +435,8 @@
                 code_scale_ref[i * group + k] = scale
                 for s in range(segments):
                     code_ref[i * group + k, :, s * LANES : (s + 1) * LANES] = codes[s][k * share : (k + 1) * share]
-        loop(1, count_x, lambda i: start(outward, i))
+        for i in range(1, count_x):
+            start(outward, i)
     sides_ref[gx] = code_ref[gx]
     sides_scale_ref[gx] = code_scale_ref[gx]
 
@@ -425,7 +444,7 @@
         flatten()
     for s in range(segments):
         lanes = slice(s * LANES, (s + 1) * LANES)
-        rhs_ref[...] = jnp.dot(place_ref[s], flat_ref[:, : last * LANES], preferred_element_type=F32)
+        rhs_ref[...] = jnp.dot(place_ref[s * rows_y : (s + 1) * rows_y], flat_ref[:, : last * LANES], preferred_element_type=F32)
 
         def solve(i):
             at = pl.ds(pl.multiple_of(i * 8, 8), 8)
@@ -442,7 +461,8 @@
 
         loop(0, rows_y // 8, solve, unroll=2)
 
-    loop(1, count_x, lambda i: finish(outward, i))
+    for i in range(1, count_x):
+        finish(outward, i)
 
     most = jnp.full((share, LANES), 0.0, F32)
     for s in range(segments):
@@ -478,16 +498,16 @@
                 solved_ref[d, :, lanes], solved_ref[jnp.maximum(d - 1, 0), :, lanes] * before, inverse
             )
 
-    def home_and_start(i):
-        home_code(partner(gx, i, count_x))
+    for i in range(1, count_x):
+        home_code(to_x(i))
         start(homeward, i)
-
-    loop(1, count_x, home_and_start)
     home_code(gx)
     back_ref[gx] = home_ref[gx]
     back_scale_ref[gx] = home_scale_ref[gx]
-    loop(1, devices, lambda i: tile_copy(i, came(i)).wait_send())
-    loop(1, count_x, lambda i: finish(homeward, i))
+    for i in range(1, devices):
+        tile_copy(i, came(i)).wait_send()
+    for i in range(1, count_x):
+        finish(homeward, i)
 
 
 def step(viscosity, forces, weights, owner, slots, velocity, grid_x, grid_y, capacity):
@@ -496,7 +516,7 @@
     devices = grid_x * grid_y
     rows = devices * capacity
     share = cells_y // grid_x
-    chunks = 4
+    chunks = 2
     dma = pltpu.SemaphoreType.DMA
     vmem = pltpu.VMEM
     anywhere = pl.BlockSpec(memory_space=pl.ANY)
@@ -529,7 +549,7 @@
             vmem((devices, capacity, cells), BF16),
             vmem((devices, 1, LANES), F32),
             vmem((devices, 1, LANES), F32),
-            vmem((cells_z // LANES, cells_y, rows), BF16),
+            vmem((cells_z // LANES * cells_y, rows), BF16),
             vmem((rows, 2 * LANES), F32),
             vmem((2, cells_y, cells_z), F32),
             vmem((2 * cells_x, 8, LANES), F32),
@@ -577,10 +597,15 @@
     return jnp.concatenate(parts, axis=0)
 
 
-def final_kernel(inner_ref, back_ref, scale_ref, mix_ref, out_ref):
+def final_kernel(parts, inner_ref, back_ref, scale_ref, mix_ref, out_hbm, out_ref, sem):
     count, rows_y, cells_z = inner_ref.shape
-
-    def chunk(i, carry):
+    rows = rows_y // parts
+
+    def copy(p):
+        at = pl.ds(pl.multiple_of(p * rows, 8), rows)
+        return pltpu.make_async_copy(out_ref.at[:, at, :], out_hbm.at[:, at, :], sem.at[p])
+
+    def chunk(i):
         at = pl.ds(pl.multiple_of(i * 8, 8), 8)
         codes = rows_of(back_ref, i)
         scale = scale_of(scale_ref, i, back_ref.shape[1])
@@ -592,27 +617,31 @@
                     inner_ref[x, at, lane] + mix_ref[x] * before + mix_ref[count + x] * last
                 )
             out_ref[count, at, lane] = last
+
+    def part(p, carry):
+        for k in range(rows // 8):
+            chunk(p * (rows // 8) + k)
+        copy(p).start()
         return carry
 
-    lax.fori_loop(0, rows_y // 8, chunk, 0)
+    def done(p, carry):
+        copy(p).wait()
+        return carry
+
+    lax.fori_loop(0, parts, part, 0)
+    lax.fori_loop(0, parts, done, 0)
 
 
 def final(inner, back, scale, mix):
     count, cells_y, cells_z = inner.shape
-    parts = 4
-    rows = cells_y // parts
-    peers = back.shape[0] // parts
+    parts = 8
+    shape = (count + 1, cells_y, cells_z)
     return pl.pallas_call(
-        final_kernel,
-        out_shape=jax.ShapeDtypeStruct((count + 1, cells_y, cells_z), F32),
-        grid=(parts,),
-        in_specs=[
-            pl.BlockSpec((count, rows, cells_z), lambda i: (0, i, 0)),
-            pl.BlockSpec((peers,) + back.shape[1:], lambda i: (i, 0, 0)),
-            pl.BlockSpec((peers,) + scale.shape[1:], lambda i: (i, 0, 0)),
-            pl.BlockSpec(mix.shape, lambda i: (0, 0, 0)),
-        ],
-        out_specs=pl.BlockSpec((count + 1, rows, cells_z), lambda i: (0, i, 0)),
+        functools.partial(final_kernel, parts),
+        out_shape=jax.ShapeDtypeStruct(shape, F32),
+        in_specs=[pl.BlockSpec(memory_space=pltpu.VMEM)] * 4,
+        out_specs=pl.BlockSpec(memory_space=pl.ANY),
+        scratch_shapes=[pltpu.VMEM(shape, F32), pltpu.SemaphoreType.DMA((parts,))],
         compiler_params=pltpu.CompilerParams(vmem_limit_bytes=24 << 20),
     )(inner, back, scale, mix)
 

time: 58 us -> 54.5 us (0.940)
  Pallas kernels: 57.9 us -> 54.3 us
    pallas_call x1, Pallas kernels: 54.9 us -> 52.1 us  [step(): pl.pallas_call(functools.partial(step_kernel, grid_x, grid_y, capacity, c...]
    pallas_call x1, Pallas kernels: 2.97 us -> 2.19 us  [final(): pl.pallas_call(functools.partial(final_kernel, parts), out_shape=jax.Shap...]
where the time goes in v2:
time: 54.5 us; the launch traced here: 54.3 us
  Pallas kernels  54.3 us (100%)
    pallas_call x1, Pallas kernels, step(): pl.pallas_call(functools.partial(step_kernel, grid_x, grid_y, capacity, c...  52.1 us
    pallas_call x1, Pallas kernels, final(): pl.pallas_call(functools.partial(final_kernel, parts), out_shape=jax.Shap...  2.19 us

profile of v2, /device:TPU:0, one launch (start us, length us, event | category | flops | bytes accessed | tf_op | source)
XLA Modules:
  0.0 54.3 jit_solution(8593832136680073763)
XLA Ops:
  0.0 52.1 %shard_map.64 = (f32[15,128,512]{2,1,0:T(8,128)S(1)}, s32[16,8,512]{2,1,0:T(8,128)S(1)}, f32[16,1,128]{2,1,0:T(1,128)S(1)}, f32[30,8,128]{2,1,0:T(8,128)S(1)}) custom-call(f32[16]{0:T(128)} %visc_hbm.1, bf16[16,128]{1,0:T(8,128)(2,1)} %bitcast.3, bf16[128,16,2048]{2,1,0:T(8,128)(2,1)} %weights_hbm.1, s32[1,128]{1,0:T(1,128)} %bitcast.4, s32[1,128]{1,0:T(1,128)} %bitcast.5, ...), custom_call_target="tpu_custom_call" | custom-call | tf_op jit(solution)/shard_map/pallas_call | solution.py:530
  52.1 2.2 %shard_map.65 = f32[16,128,512]{2,1,0:T(8,128)} custom-call(f32[15,128,512]{2,1,0:T(8,128)S(1)} %get-tuple-element.9.inner_ref, s32[16,8,512]{2,1,0:T(8,128)S(1)} %get-tuple-element.10.back_ref, f32[16,1,128]{2,1,0:T(1,128)S(1)} %get-tuple-element.11.scale_ref, f32[30,8,128]{2,1,0:T(8,128)S(1)} %get-tuple-element.12.mix_ref), custom_call_target="tpu_custom_call" | custom-call | tf_op jit(solution)/shard_map/pallas_call | solution.py:639

commit v3 on v2

--- a/solution.py
+++ b/solution.py
@@ -142,17 +142,16 @@
     spread_ref, outgoing_ref, tiles_ref, meta_ref, metas_ref, place_ref, tile_ends_ref, ends_ref,
     local_ref, weight_ref, couple_ref, code_ref, code_scale_ref, sides_ref, sides_scale_ref,
     solved_ref, home_ref, home_scale_ref, rhs_ref, flat_ref,
-    own, wsem, tile_send, tile_recv, meta_send, meta_recv,
-    code_send, code_recv, cscale_send, cscale_recv, home_send, home_recv, hscale_send, hscale_recv,
+    own, wsem, tile_send, tile_recv, meta_sem, line_sem,
 ):
     devices = count_x * count_y
     cells_x, rows_y, cells_z = velocity_ref.shape
     markers, blocks = forces_ref.shape
-    cells = outgoing_ref.shape[2]
+    width = outgoing_ref.shape[3]
+    cells = chunks * width
     wide = blocks * markers
     rows = devices * capacity
     share = code_ref.shape[1]
-    width = cells // chunks
     segments = cells_z // LANES
     last = cells_x - 1
     gx, gy = lax.axis_index("gx"), lax.axis_index("gy")
@@ -200,7 +199,6 @@
 
     loop(0, chunks, lambda c: weight_copy(c).start())
     velocity_copy = pltpu.make_async_copy(velocity_hbm, velocity_ref, own.at[4])
-    velocity_copy.start()
     for copy in small:
         copy.wait()
 
@@ -230,44 +228,55 @@
     for d in range(devices):
         meta_ref[d] = meta[d : d + 1]
 
-    def spread_chunk(c):
+    def remote(source, target, send, receive, peer):
+        return pltpu.make_async_remote_copy(
+            src_ref=source,
+            dst_ref=target,
+            send_sem=send,
+            recv_sem=receive,
+            device_id=peer,
+            device_id_type=pl.DeviceIdType.MESH,
+        )
+
+    def several(source, target, send, receive, number):
+        at = pl.ds(0, number)
+        return remote(source.at[at], target.at[at], send, receive, device(1))
+
+    span = max(1, devices // 4)
+
+    def tile_copy(c, i):
+        return remote(
+            outgoing_ref.at[index(i), c], tiles_ref.at[me, c],
+            tile_send.at[0], tile_recv.at[i // span], device(i),
+        )
+
+    def tiles_come(group):
+        number = span if group else span - 1
+        several(outgoing_ref, tiles_ref, tile_send.at[0], tile_recv.at[group], number).wait_recv()
+
+    def meta_copy(i):
+        return remote(
+            meta_ref.at[index(i)], metas_ref.at[me], meta_sem.at[0], meta_sem.at[1], device(i)
+        )
+
+    for c in range(chunks):
         weight_copy(c).wait()
-        at = pl.ds(pl.multiple_of(c * width, width), width)
         out = jnp.dot(
             spread_ref[...], weights_ref[c].reshape(wide, width), preferred_element_type=F32
         )
         if capacity % 8 == 0:
-            outgoing_ref[:, :, at] = out.reshape(devices, capacity, width).astype(BF16)
+            outgoing_ref[:, c] = out.reshape(devices, capacity, width).astype(BF16)
         else:
             for d in range(devices):
-                outgoing_ref[d, :, at] = out[d * capacity : (d + 1) * capacity].astype(BF16)
-
-    loop(0, chunks, spread_chunk)
-
-    def remote(source, target, sends, receives, i, peer):
-        return pltpu.make_async_remote_copy(
-            src_ref=source,
-            dst_ref=target,
-            send_sem=sends.at[i],
-            recv_sem=receives.at[i],
-            device_id=peer,
-            device_id_type=pl.DeviceIdType.MESH,
-        )
-
-    def tile_copy(i, slot):
-        peer = index(i)
-        return remote(outgoing_ref.at[peer], tiles_ref.at[slot], tile_send, tile_recv, i, device(i))
-
-    def meta_copy(i, slot):
-        peer = index(i)
-        return remote(meta_ref.at[peer], metas_ref.at[slot], meta_send, meta_recv, i, device(i))
-
-    pl.semaphore_wait(barrier, devices - 1)
-    for i in range(1, devices):
-        meta_copy(i, me).start()
-    for i in range(1, devices):
-        tile_copy(i, me).start()
-    tiles_ref[me] = outgoing_ref[me]
+                outgoing_ref[d, c] = out[d * capacity : (d + 1) * capacity].astype(BF16)
+        if c == 0:
+            pl.semaphore_wait(barrier, devices - 1)
+            for i in range(1, devices):
+                meta_copy(i).start()
+        for i in range(1, devices):
+            tile_copy(c, i).start()
+        tiles_ref[me, c] = outgoing_ref[me, c]
+    velocity_copy.start()
     metas_ref[me] = meta_ref[me]
 
     visc = [jnp.full((8, LANES), visc_ref[x], F32) for x in range(cells_x)]
@@ -305,8 +314,7 @@
 
     loop(0, rows_y // 8, velocity_ends)
 
-    for i in range(1, devices):
-        meta_copy(i, came(i)).wait()
+    several(meta_ref, metas_ref, meta_sem.at[0], meta_sem.at[1], devices - 1).wait()
     metas = jnp.concatenate([metas_ref[d] for d in range(devices)], axis=0)
     couple(
         [
@@ -333,28 +341,37 @@
             iota((rows_y, rows), 0) * segments + s == number
         ).astype(BF16)
 
+    def tile_cells(slot, x):
+        c, lane = divmod(x * LANES, width)
+        return tiles_ref[slot, c, :, lane : lane + LANES].astype(F32)
+
     def tile_ends(slot):
         at = pl.ds(pl.multiple_of(slot * capacity, capacity), capacity)
-        high, low = ends_of(lambda x: tiles_ref[slot, :, x * LANES : (x + 1) * LANES].astype(F32))
+        high, low = ends_of(lambda x: tile_cells(slot, x))
         tile_ends_ref[at, :LANES] = high
         tile_ends_ref[at, LANES:] = low
 
     def flatten():
-        if capacity % 8 == 0:
-            flat_ref[...] = tiles_ref[...].astype(F32).reshape(rows, cells).astype(BF16)
-        else:
-            parts = [tiles_ref[d].astype(F32) for d in range(devices)]
-            flat_ref[...] = jnp.concatenate(parts, axis=0).astype(BF16)
+        for c in range(chunks):
+            at = slice(c * width, (c + 1) * width)
+            if capacity % 8 == 0:
+                flat_ref[:, at] = tiles_ref[:, c].astype(F32).reshape(rows, width).astype(BF16)
+            else:
+                parts = [tiles_ref[d, c].astype(F32) for d in range(devices)]
+                flat_ref[:, at] = jnp.concatenate(parts, axis=0).astype(BF16)
 
     if capacity % 8 == 0:
         tile_ends(me)
 
-        for i in range(1, devices):
-            tile_copy(i, came(i)).wait_recv()
-            tile_ends(came(i))
+        for group in range(devices // span):
+            if group or span > 1:
+                tiles_come(group)
+            for i in range(max(1, group * span), (group + 1) * span):
+                tile_ends(came(i))
     else:
-        for i in range(1, devices):
-            tile_copy(i, came(i)).wait_recv()
+        for group in range(devices // span):
+            if group or span > 1:
+                tiles_come(group)
         flatten()
 
         def flat_ends(i):
@@ -378,20 +395,19 @@
                 part[:, w * LANES : (w + 1) * LANES] + part[:, (w + 2) * LANES : (w + 3) * LANES]
             )
 
-    def line_copy(source, target, sends, receives, i, slot):
+    outward = ((code_ref, sides_ref, 0), (code_scale_ref, sides_scale_ref, 2))
+    homeward = ((home_ref, back_ref, 4), (home_scale_ref, back_scale_ref, 6))
+
+    def start(groups, i):
         peer = to_x(i)
-        return remote(source.at[peer], target.at[slot], sends, receives, i, (peer, gy))
-
-    outward = ((code_ref, sides_ref, code_send, code_recv), (code_scale_ref, sides_scale_ref, cscale_send, cscale_recv))
-    homeward = ((home_ref, back_ref, home_send, home_recv), (home_scale_ref, back_scale_ref, hscale_send, hscale_recv))
-
-    def start(groups, i):
-        for group in groups:
-            line_copy(*group, i, gx).start()
-
-    def finish(groups, i):
-        for group in groups:
-            line_copy(*group, i, from_x(i)).wait()
+        for source, target, k in groups:
+            remote(
+                source.at[peer], target.at[gx], line_sem.at[k], line_sem.at[k + 1], (peer, gy)
+            ).start()
+
+    def finish(groups):
+        for source, target, k in groups:
+            several(source, target, line_sem.at[k], line_sem.at[k + 1], count_x - 1).wait()
 
     def code_rows(i):
         at = pl.ds(pl.multiple_of(i * 8, 8), 8)
@@ -461,8 +477,7 @@
 
         loop(0, rows_y // 8, solve, unroll=2)
 
-    for i in range(1, count_x):
-        finish(outward, i)
+    finish(outward)
 
     most = jnp.full((share, LANES), 0.0, F32)
     for s in range(segments):
@@ -504,10 +519,8 @@
     home_code(gx)
     back_ref[gx] = home_ref[gx]
     back_scale_ref[gx] = home_scale_ref[gx]
-    for i in range(1, devices):
-        tile_copy(i, came(i)).wait_send()
-    for i in range(1, count_x):
-        finish(homeward, i)
+    several(outgoing_ref, tiles_ref, tile_send.at[0], tile_recv.at[0], devices - 1).wait_send()
+    finish(homeward)
 
 
 def step(viscosity, forces, weights, owner, slots, velocity, grid_x, grid_y, capacity):
@@ -516,7 +529,7 @@
     devices = grid_x * grid_y
     rows = devices * capacity
     share = cells_y // grid_x
-    chunks = 2
+    chunks = 4
     dma = pltpu.SemaphoreType.DMA
     vmem = pltpu.VMEM
     anywhere = pl.BlockSpec(memory_space=pl.ANY)
@@ -545,8 +558,8 @@
             vmem((chunks, blocks, markers, cells // chunks), BF16),
             vmem((cells_x, cells_y, cells_z), F32),
             vmem((rows, blocks * markers), BF16),
-            vmem((devices, capacity, cells), BF16),
-            vmem((devices, capacity, cells), BF16),
+            vmem((devices, chunks, capacity, cells // chunks), BF16),
+            vmem((devices, chunks, capacity, cells // chunks), BF16),
             vmem((devices, 1, LANES), F32),
             vmem((devices, 1, LANES), F32),
             vmem((cells_z // LANES * cells_y, rows), BF16),
@@ -566,12 +579,11 @@
             vmem((rows, cells), BF16),
             dma((5,)),
             dma((chunks,)),
-            dma((devices,)),
-            dma((devices,)),
-            dma((devices,)),
-            dma((devices,)),
-        ]
-        + [dma((grid_x,))] * 8,
+            dma((1,)),
+            dma((4,)),
+            dma((2,)),
+            dma((8,)),
+        ],
         compiler_params=pltpu.CompilerParams(
             collective_id=0, has_side_effects=True, vmem_limit_bytes=40 << 20
         ),

time: 54.5 us -> 50.8 us (0.932)
  Pallas kernels: 54.3 us -> 50.6 us
    pallas_call x1, Pallas kernels: 52.1 us -> 48.4 us  [step(): pl.pallas_call(functools.partial(step_kernel, grid_x, grid_y, capacity, c...]
where the time goes in v3:
time: 50.8 us; the launch traced here: 50.6 us
  Pallas kernels  50.6 us (100%)
    pallas_call x1, Pallas kernels, step(): pl.pallas_call(functools.partial(step_kernel, grid_x, grid_y, capacity, c...  48.4 us
    pallas_call x1, Pallas kernels, final(): pl.pallas_call(functools.partial(final_kernel, parts), out_shape=jax.Shap...  2.19 us

profile of v3, /device:TPU:0, one launch (start us, length us, event | category | flops | bytes accessed | tf_op | source)
XLA Modules:
  0.0 50.6 jit_solution(16632983660522185795)
XLA Ops:
  0.0 48.4 %shard_map.64 = (f32[15,128,512]{2,1,0:T(8,128)S(1)}, s32[16,8,512]{2,1,0:T(8,128)S(1)}, f32[16,1,128]{2,1,0:T(1,128)S(1)}, f32[30,8,128]{2,1,0:T(8,128)S(1)}) custom-call(f32[16]{0:T(128)} %visc_hbm.1, bf16[16,128]{1,0:T(8,128)(2,1)} %bitcast.3, bf16[128,16,2048]{2,1,0:T(8,128)(2,1)} %weights_hbm.1, s32[1,128]{1,0:T(1,128)} %bitcast.4, s32[1,128]{1,0:T(1,128)} %bitcast.5, ...), custom_call_target="tpu_custom_call" | custom-call | tf_op jit(solution)/shard_map/pallas_call | solution.py:543
  48.4 2.2 %shard_map.65 = f32[16,128,512]{2,1,0:T(8,128)} custom-call(f32[15,128,512]{2,1,0:T(8,128)S(1)} %get-tuple-element.9.inner_ref, s32[16,8,512]{2,1,0:T(8,128)S(1)} %get-tuple-element.10.back_ref, f32[16,1,128]{2,1,0:T(1,128)S(1)} %get-tuple-element.11.scale_ref, f32[30,8,128]{2,1,0:T(8,128)S(1)} %get-tuple-element.12.mix_ref), custom_call_target="tpu_custom_call" | custom-call | tf_op jit(solution)/shard_map/pallas_call | solution.py:651

commit v4 on v3

--- a/solution.py
+++ b/solution.py
@@ -271,10 +271,11 @@
                 outgoing_ref[d, c] = out[d * capacity : (d + 1) * capacity].astype(BF16)
         if c == 0:
             pl.semaphore_wait(barrier, devices - 1)
+        for i in range(1, devices):
+            tile_copy(c, i).start()
+        if c == 0:
             for i in range(1, devices):
                 meta_copy(i).start()
-        for i in range(1, devices):
-            tile_copy(c, i).start()
         tiles_ref[me, c] = outgoing_ref[me, c]
     velocity_copy.start()
     metas_ref[me] = meta_ref[me]

time: 50.8 us -> 50.7 us (level)
  no operation moved by 1% of the time
where the time goes in v4:
time: 50.7 us; the launch traced here: 50.5 us
  Pallas kernels  50.5 us (100%)
    pallas_call x1, Pallas kernels, step(): pl.pallas_call(functools.partial(step_kernel, grid_x, grid_y, capacity, c...  48.3 us
    pallas_call x1, Pallas kernels, final(): pl.pallas_call(functools.partial(final_kernel, parts), out_shape=jax.Shap...  2.19 us

profile of v4, /device:TPU:0, one launch (start us, length us, event | category | flops | bytes accessed | tf_op | source)
XLA Modules:
  0.0 50.5 jit_solution(14385496038969939462)
XLA Ops:
  0.0 48.3 %shard_map.64 = (f32[15,128,512]{2,1,0:T(8,128)S(1)}, s32[16,8,512]{2,1,0:T(8,128)S(1)}, f32[16,1,128]{2,1,0:T(1,128)S(1)}, f32[30,8,128]{2,1,0:T(8,128)S(1)}) custom-call(f32[16]{0:T(128)} %visc_hbm.1, bf16[16,128]{1,0:T(8,128)(2,1)} %bitcast.3, bf16[128,16,2048]{2,1,0:T(8,128)(2,1)} %weights_hbm.1, s32[1,128]{1,0:T(1,128)} %bitcast.4, s32[1,128]{1,0:T(1,128)} %bitcast.5, ...), custom_call_target="tpu_custom_call" | custom-call | tf_op jit(solution)/shard_map/pallas_call | solution.py:544
  48.3 2.2 %shard_map.65 = f32[16,128,512]{2,1,0:T(8,128)} custom-call(f32[15,128,512]{2,1,0:T(8,128)S(1)} %get-tuple-element.9.inner_ref, s32[16,8,512]{2,1,0:T(8,128)S(1)} %get-tuple-element.10.back_ref, f32[16,1,128]{2,1,0:T(1,128)S(1)} %get-tuple-element.11.scale_ref, f32[30,8,128]{2,1,0:T(8,128)S(1)} %get-tuple-element.12.mix_ref), custom_call_target="tpu_custom_call" | custom-call | tf_op jit(solution)/shard_map/pallas_call | solution.py:652
